TPU v7x, 32 devices: a whole 2x2x4 slice. The times are simulated.
32 devices in a mesh: groups: 2 (over x), gx: 8 (over z, y), gy: 2 (over core).
Axes of the slice: x: 2, y: 2, z: 4, core: 2. Of those that a mesh axis runs over, the one named last changes fastest.
Arguments:
- source: float32 [2, 3, 2, 32, 64, 256], P('groups', None, None, 'gx', 'gy'), parts along dimension 0, may hold values from -12 to 12
- permittivity: float32 [6, 32, 64, 256], P('groups', 'gx', 'gy'), parts along dimension 0, may hold values from 1 to 12
- frequency: float32 [1], replicated, may hold values from 0.25 to 0.6
Outputs:
- solution: float32 [2, 3, 2, 32, 64, 256], P('groups', None, None, 'gx', 'gy'), parts along dimension 0
- residual: float32 [2, 3, 2, 32, 64, 256], P('groups', None, None, 'gx', 'gy'), parts along dimension 0
There are 2 independent parts, one for each index of `groups`. A program takes and returns all parts, laid end to end along the dimension named above; an argument that names none is the same for every part. Nothing has to cross between parts.
All inputs are finite; a program needn't handle non-finite values.
Results may differ from a plain program's by a relative error of at most 0.0003.
Values sent between devices are 32-bit elements; how exact they have to be, the bound alone decides.
A program may use at most 64 MiB of HBM per device.

v0:
```python
import jax
import jax.numpy as jnp
from jax import lax
from jax.sharding import PartitionSpec as P

NZ = 256
PML = 8
ITERS = 3
pml_strength = 2.0


def shifted(array, axis, by):
    devices = lax.axis_size(axis)
    pairs = [(i, i + by) for i in range(devices) if 0 <= i + by < devices]
    return lax.ppermute(array, axis, pairs)


def stretch(points, length, frequency):
    inside = jnp.maximum(jnp.maximum(PML - points, points - (length - PML)), 0.0) / PML
    damping = pml_strength * inside**3 / frequency[:, None]
    factor = 1.0 / (1.0 + damping * damping)
    return jnp.stack([factor, -damping * factor], axis=1)


def orient(coefficient, dimension):
    target = [coefficient.shape[0], 2, 1, 1, 1]
    target[dimension] = coefficient.shape[2]
    return coefficient.reshape(target)


def times_coef(values, coefficient):
    real_part = values[:, 0] * coefficient[:, 0] - values[:, 1] * coefficient[:, 1]
    imag_part = values[:, 0] * coefficient[:, 1] + values[:, 1] * coefficient[:, 0]
    return jnp.stack([real_part, imag_part], axis=1)


def curl_forward(extended, front_x, front_y, front_z):
    centre = extended[:, :, :, :-1, :-1]

    def step_x(component):
        return extended[:, component, :, 1:, :-1] - centre[:, component]

    def step_y(component):
        return extended[:, component, :, :-1, 1:] - centre[:, component]

    def step_z(component):
        cells = centre[:, component]
        above = jnp.concatenate([cells[..., 1:], jnp.zeros_like(cells[..., :1])], axis=-1)
        return above - cells

    curl_x = times_coef(step_y(2), front_y) - times_coef(step_z(1), front_z)
    curl_y = times_coef(step_z(0), front_z) - times_coef(step_x(2), front_x)
    curl_z = times_coef(step_x(1), front_x) - times_coef(step_y(0), front_y)
    return jnp.stack([curl_x, curl_y, curl_z], axis=1)


def curl_backward(padded, back_x, back_y, back_z):
    centre = padded[:, :, :, 1:, 1:]

    def step_x(component):
        return centre[:, component] - padded[:, component, :, :-1, 1:]

    def step_y(component):
        return centre[:, component] - padded[:, component, :, 1:, :-1]

    def step_z(component):
        cells = centre[:, component]
        below = jnp.concatenate([jnp.zeros_like(cells[..., :1]), cells[..., :-1]], axis=-1)
        return cells - below

    out_x = times_coef(step_y(2), back_y) - times_coef(step_z(1), back_z)
    out_y = times_coef(step_z(0), back_z) - times_coef(step_x(2), back_x)
    out_z = times_coef(step_x(1), back_x) - times_coef(step_y(0), back_y)
    return jnp.stack([out_x, out_y, out_z], axis=1)


def scaled(values, number):
    real_scale = number[0].reshape(-1, 1, 1, 1, 1)
    imag_scale = number[1].reshape(-1, 1, 1, 1, 1)
    real_part = values[:, :, 0] * real_scale - values[:, :, 1] * imag_scale
    imag_part = values[:, :, 0] * imag_scale + values[:, :, 1] * real_scale
    return jnp.stack([real_part, imag_part], axis=2)


def product(left, right):
    real_part = jnp.sum(
        left[:, :, 0] * right[:, :, 0] + left[:, :, 1] * right[:, :, 1], axis=(1, 2, 3, 4)
    )
    imag_part = jnp.sum(
        left[:, :, 0] * right[:, :, 1] - left[:, :, 1] * right[:, :, 0], axis=(1, 2, 3, 4)
    )
    return jnp.stack([real_part, imag_part])


def complex_times(first, other):
    return jnp.stack(
        [first[0] * other[0] - first[1] * other[1], first[0] * other[1] + first[1] * other[0]]
    )


def complex_ratio(first, other):
    modulus = other[0] * other[0] + other[1] * other[1]
    return (
        jnp.stack(
            [first[0] * other[0] + first[1] * other[1], first[1] * other[0] - first[0] * other[1]]
        )
        / modulus
    )


def grid_points(start, first, count):
    return (start + jnp.arange(first, count, dtype=jnp.int32)).astype(jnp.float32)


def body(source, permittivity, frequency):
    cells_x = source.shape[3]
    cells_y = source.shape[4]
    total_x = cells_x * lax.axis_size("gx")
    total_y = cells_y * lax.axis_size("gy")
    index_x = lax.axis_index("gx")
    index_y = lax.axis_index("gy")
    margin = 0
    front_x = orient(
        stretch(grid_points(index_x * cells_x, -margin, cells_x) + 0.5, total_x, frequency), 2
    )
    front_y = orient(
        stretch(grid_points(index_y * cells_y, -margin, cells_y) + 0.5, total_y, frequency), 3
    )
    back_x = orient(stretch(grid_points(index_x * cells_x, 0, cells_x), total_x, frequency), 2)
    back_y = orient(stretch(grid_points(index_y * cells_y, 0, cells_y), total_y, frequency), 3)
    z_points = grid_points(0, 0, NZ)
    front_z = orient(stretch(z_points + 0.5, NZ, frequency), 4)
    back_z = orient(stretch(z_points, NZ, frequency), 4)
    material = (frequency * frequency).reshape(-1, 1, 1, 1, 1, 1) * permittivity[None, :, None]

    def operate(values):
        above_x = shifted(values[:, :, :, :1], "gx", -1)
        above_y = shifted(values[:, :, :, :, :1], "gy", -1)
        extended = jnp.concatenate([values, above_x], axis=3)
        side_cells = jnp.concatenate([above_y, jnp.zeros_like(above_y[:, :, :, :1])], axis=3)
        extended = jnp.concatenate([extended, side_cells], axis=4)
        rotated = curl_forward(extended, front_x, front_y, front_z)
        below_x = shifted(rotated[:, :, :, -1:], "gx", 1)
        below_y = shifted(rotated[:, :, :, :, -1:], "gy", 1)
        padded = jnp.concatenate([below_x, rotated], axis=3)
        side_cells = jnp.concatenate([jnp.zeros_like(below_y[:, :, :, :1]), below_y], axis=3)
        padded = jnp.concatenate([side_cells, padded], axis=4)
        applied = curl_backward(padded, back_x, back_y, back_z)
        return applied - material * values

    solution = jnp.zeros_like(source)
    residual = source
    direction = source
    shadow_dot = lax.psum(product(source, residual), ("gx", "gy"))
    for iteration in range(ITERS):
        applied = operate(direction)
        step_size = complex_ratio(shadow_dot, lax.psum(product(source, applied), ("gx", "gy")))
        middle = residual - scaled(applied, step_size)
        second = operate(middle)
        sums_triple = lax.psum(
            (product(second, middle), product(second, second), product(source, second)),
            ("gx", "gy"),
        )
        weight = complex_ratio(sums_triple[0], sums_triple[1])
        solution = solution + scaled(direction, step_size) + scaled(middle, weight)
        residual = middle - scaled(second, weight)
        if iteration + 1 < ITERS:
            shadow_next = -complex_times(weight, sums_triple[2])
            momentum = complex_times(
                complex_ratio(shadow_next, shadow_dot), complex_ratio(step_size, weight)
            )
            direction = residual + scaled(direction - scaled(applied, weight), momentum)
            shadow_dot = shadow_next
    return (solution, residual)


def solution(mesh):
    placed = (P("groups", None, None, "gx", "gy", None), P("groups", "gx", "gy", None), P())
    return jax.shard_map(
        body,
        mesh=mesh,
        in_specs=placed,
        out_specs=(
            P("groups", None, None, "gx", "gy", None),
            P("groups", None, None, "gx", "gy", None),
        ),
        check_vma=False,
    )
```

profile of v0, /device:TPU:0, one launch (start us, length us, event | category | flops | bytes accessed | tf_op | source)
XLA Modules:
  0.0 469.3 jit_solution(13969787863053648633)
XLA Ops:
  7.5 6.7 %collective-permute-done = f32[1,3,2,1,32,256]{5,4,3,2,1,0:T(8,128)S(1)} collective-permute-done((f32[1,3,2,1,32,256]{5,4,3,2,1,0:T(8,128)S(1)}, f32[1,3,2,1,32,256]{5,4,3,2,1,0:T(8,128)S(1)}, u32[]{:S(2)}, u32[]{:S(2)}) %collective-permute-start) | collective-permute-done | bytes 196640 | tf_op jit(solution)/shard_map/ppermute | solution.py:15
  15.4 2.2 collective-permute-start.2
  17.5 5.0 %collective-permute-start.3 = (f32[1,3,2,1,32,256]{5,4,3,2,1,0:T(8,128)S(1)}, f32[1,3,2,1,32,256]{5,4,3,2,1,0:T(8,128)S(1)}, u32[]{:S(2)}, u32[]{:S(2)}) collective-permute-start(f32[1,3,2,1,32,256]{5,4,3,2,1,0:T(8,128)S(1)} %pad_maximum_fusion.33), channel_id=1, source_target_pairs={{0,2},{2,4},{4,6},{6,8},{8,10},{10,12},{12,14},{1,3},{3,5},{5,7},{... | collective-permute-start | bytes 589832 | tf_op jit(solution)/shard_map/ppermute | solution.py:15
  22.5 3.6 collective-permute-done.3
  31.1 31.3 %all-reduce.39 = (f32[2,1]{1,0:T(2,128)S(1)}, f32[2,1]{1,0:T(2,128)S(1)}) all-reduce(f32[2,1]{1,0:T(2,128)S(1)} %pad_maximum_fusion.41, f32[2,1]{1,0:T(2,128)S(1)} %pad_maximum_fusion.42), channel_id=1, replica_groups=mesh['groups'=2,'gx'=8,'gy'=2] {'gx','gy'}, use_global_device_ids=true, to_apply=%region_2.0 | all-reduce | flops 4 | bytes 32 | tf_op jit(solution)/shard_map/psum | solution.py:154
  77.4 3.2 collective-permute-done.4
  94.9 29.5 %all-reduce.38 = (f32[2,1]{1,0:T(2,128)S(1)}, f32[2,1]{1,0:T(2,128)S(1)}, f32[2,1]{1,0:T(2,128)S(1)}) all-reduce(f32[2,1]{1,0:T(2,128)S(1)} %pad_maximum_fusion.43, f32[2,1]{1,0:T(2,128)S(1)} %pad_maximum_fusion.44, f32[2,1]{1,0:T(2,128)S(1)} %pad_maximum_fusion.45), channel_id=1, replica_groups=mesh['groups'=2,'gx'=8,'gy'=2] {'gx','gy'}, use_global_device_ids=true, to_apply=%region_8.0 | all-reduce | flops 6 | bytes 48 | tf_op jit(solution)/shard_map/psum | solution.py:160
  141.5 2.5 multiply_subtract_fusion.11
  166.5 1.8 collective-permute-done.9
  168.3 4.2 collective-permute-done.8
  183.4 30.3 %psum.89 = f32[2,1]{1,0:T(2,128)S(1)} all-reduce(f32[2,1]{1,0:T(2,128)S(1)} %pad_maximum_fusion.46), channel_id=1, replica_groups=mesh['groups'=2,'gx'=8,'gy'=2] {'gx','gy'}, use_global_device_ids=true, to_apply=%region_17.0 | all-reduce | flops 2 | bytes 16 | tf_op jit(solution)/shard_map/psum | solution.py:157
  222.7 2.5 multiply_subtract_fusion.8
  230.0 3.4 collective-permute-done.12
  247.5 1.9 pad_maximum_fusion.48
  249.4 1.9 pad_maximum_fusion.47
  251.3 30.6 %all-reduce.37 = (f32[2,1]{1,0:T(2,128)}, f32[2,1]{1,0:T(2,128)}, f32[2,1]{1,0:T(2,128)}) all-reduce(f32[2,1]{1,0:T(2,128)} %pad_maximum_fusion.47, f32[2,1]{1,0:T(2,128)} %pad_maximum_fusion.48, f32[2,1]{1,0:T(2,128)} %pad_maximum_fusion.49), channel_id=1, replica_groups=mesh['groups'=2,'gx'=8,'gy'=2] {'gx','gy'}, use_global_device_ids=true, to_apply=%region_20.0 | all-reduce | flops 6 | bytes 48 | tf_op jit(solution)/shard_map/psum | solution.py:160
  300.1 2.5 multiply_subtract_fusion.5
  327.7 3.7 collective-permute-done.16
  342.3 3.0 add_reduce_fusion.2
  345.3 1.8 pad_maximum_fusion.50
  347.1 2.3 multiply_subtract_fusion.13
  349.4 30.0 %psum.93 = f32[2,1]{1,0:T(2,128)S(1)} all-reduce(f32[2,1]{1,0:T(2,128)} %pad_maximum_fusion.50), channel_id=1, replica_groups=mesh['groups'=2,'gx'=8,'gy'=2] {'gx','gy'}, use_global_device_ids=true, to_apply=%region_29.0 | all-reduce | flops 2 | bytes 16 | tf_op jit(solution)/shard_map/psum | solution.py:157
  388.2 2.5 multiply_subtract_fusion.2
  390.7 2.3 maximum_subtract_fusion.11
  395.6 2.3 multiply_subtract_fusion.9
  397.9 5.9 %collective-permute-done.20 = f32[1,3,2,1,32,256]{5,4,3,2,1,0:T(8,128)S(1)} collective-permute-done((f32[1,3,2,1,32,256]{5,4,3,2,1,0:T(8,128)S(1)}, f32[1,3,2,1,32,256]{5,4,3,2,1,0:T(8,128)S(1)}, u32[]{:S(2)}, u32[]{:S(2)}) %collective-permute-start.20) | collective-permute-done | bytes 196640 | tf_op jit(solution)/shard_map/ppermute | solution.py:15
  405.4 2.0 collective-permute-start.22
  407.5 1.9 collective-permute-start.23
  409.3 2.2 multiply_subtract_fusion.7
  420.7 2.2 multiply_subtract_fusion.3
  422.9 29.5 %all-reduce.36 = (f32[2,1]{1,0:T(2,128)S(1)}, f32[2,1]{1,0:T(2,128)S(1)}) all-reduce(f32[2,1]{1,0:T(2,128)S(1)} %pad_maximum_fusion.51, f32[2,1]{1,0:T(2,128)S(1)} %pad_maximum_fusion.52), channel_id=1, replica_groups=mesh['groups'=2,'gx'=8,'gy'=2] {'gx','gy'}, use_global_device_ids=true, to_apply=%region_32.0 | all-reduce | flops 4 | bytes 32 | tf_op jit(solution)/shard_map/psum | solution.py:160
  461.4 2.6 multiply_subtract_fusion
  (455 shorter events, 112.2 us)
Async XLA Ops:
  1.6 12.5 %collective-permute-start.1 = (f32[1,3,2,4,1,256]{5,4,3,2,1,0:T(1,128)S(1)}, f32[1,3,2,4,1,256]{5,4,3,2,1,0:T(1,128)S(1)}, u32[]{:S(2)}, u32[]{:S(2)}) collective-permute-start(f32[1,3,2,4,1,256]{5,4,3,2,1,0:T(1,128)S(1)} %slice.702), channel_id=1, source_target_pairs={{1,0},{3,2},{5,4},{7,6},{9,8},{11,10},{13,12},{15,14},{17,16},{19,... | collective-permute-start | bytes 73736 | tf_op jit(solution)/shard_map/ppermute | solution.py:15
  3.9 10.2 %collective-permute-start = (f32[1,3,2,1,32,256]{5,4,3,2,1,0:T(8,128)S(1)}, f32[1,3,2,1,32,256]{5,4,3,2,1,0:T(8,128)S(1)}, u32[]{:S(2)}, u32[]{:S(2)}) collective-permute-start(f32[1,3,2,1,32,256]{5,4,3,2,1,0:T(8,128)S(1)} %slice.695), channel_id=1, source_target_pairs={{2,0},{4,2},{6,4},{8,6},{10,8},{12,10},{14,12},{3,1},{5,3},{7,5},{... | collective-permute-start | bytes 589832 | tf_op jit(solution)/shard_map/ppermute | solution.py:15
  7.1 172.1 %copy-start.53 = (f32[4]{0:T(128)}, f32[4]{0:T(128)S(1)}, u32[]{:S(2)}) copy-start(f32[4]{0:T(128)S(1)} %get-tuple-element.424) | copy-start | bytes 52
  7.1 172.1 %copy-start.57 = (f32[4]{0:T(128)}, f32[4]{0:T(128)S(1)}, u32[]{:S(2)}) copy-start(f32[4]{0:T(128)S(1)} %get-tuple-element.425) | copy-start | bytes 52
  7.2 166.2 %copy-start.61 = (f32[4]{0:T(128)}, f32[4]{0:T(128)S(1)}, u32[]{:S(2)}) copy-start(f32[4]{0:T(128)S(1)} %get-tuple-element.432) | copy-start | bytes 52
  7.2 166.2 %copy-start.65 = (f32[4]{0:T(128)}, f32[4]{0:T(128)S(1)}, u32[]{:S(2)}) copy-start(f32[4]{0:T(128)S(1)} %get-tuple-element.433) | copy-start | bytes 52
  7.4 172.3 %copy-start.16 = (f32[3,4,32,256]{3,2,1,0:T(8,128)}, f32[3,4,32,256]{3,2,1,0:T(8,128)S(1)}, u32[]{:S(2)}) copy-start(f32[3,4,32,256]{3,2,1,0:T(8,128)S(1)} %broadcast_multiply_fusion) | copy-start | bytes 1179652
  7.4 165.7 %copy-start.77 = (f32[32]{0:T(128)}, f32[32]{0:T(128)S(1)}, u32[]{:S(2)}) copy-start(f32[32]{0:T(128)S(1)} %get-tuple-element.430) | copy-start | bytes 388
  7.4 165.7 %copy-start.81 = (f32[32]{0:T(128)}, f32[32]{0:T(128)S(1)}, u32[]{:S(2)}) copy-start(f32[32]{0:T(128)S(1)} %get-tuple-element.431) | copy-start | bytes 388
  15.4 7.2 %collective-permute-start.2 = (f32[1,3,2,4,1,256]{5,4,3,2,1,0:T(1,128)S(1)}, f32[1,3,2,4,1,256]{5,4,3,2,1,0:T(1,128)S(1)}, u32[]{:S(2)}, u32[]{:S(2)}) collective-permute-start(f32[1,3,2,4,1,256]{5,4,3,2,1,0:T(1,128)S(1)} %pad_maximum_fusion.40), channel_id=1, source_target_pairs={{0,1},{2,3},{4,5},{6,7},{8,9},{10,11},{12,13},{14,15},{16,17},{18,... | collective-permute-start | bytes 73736 | tf_op jit(solution)/shard_map/ppermute | solution.py:15
  17.5 8.7 %collective-permute-start.3 = (f32[1,3,2,1,32,256]{5,4,3,2,1,0:T(8,128)S(1)}, f32[1,3,2,1,32,256]{5,4,3,2,1,0:T(8,128)S(1)}, u32[]{:S(2)}, u32[]{:S(2)}) collective-permute-start(f32[1,3,2,1,32,256]{5,4,3,2,1,0:T(8,128)S(1)} %pad_maximum_fusion.33), channel_id=1, source_target_pairs={{0,2},{2,4},{4,6},{6,8},{8,10},{10,12},{12,14},{1,3},{3,5},{5,7},{... | collective-permute-start | bytes 589832 | tf_op jit(solution)/shard_map/ppermute | solution.py:15
  22.5 156.8 %copy-start.69 = (f32[32]{0:T(128)}, f32[32]{0:T(128)S(1)}, u32[]{:S(2)}) copy-start(f32[32]{0:T(128)S(1)} %get-tuple-element.422) | copy-start | bytes 388
  73.0 7.6 %collective-permute-start.4 = (f32[1,3,2,1,32,256]{5,4,3,2,1,0:T(8,128)S(1)}, f32[1,3,2,1,32,256]{5,4,3,2,1,0:T(8,128)S(1)}, u32[]{:S(2)}, u32[]{:S(2)}) collective-permute-start(f32[1,3,2,1,32,256]{5,4,3,2,1,0:T(8,128)S(1)} %slice.2127), channel_id=1, source_target_pairs={{2,0},{4,2},{6,4},{8,6},{10,8},{12,10},{14,12},{3,1},{5,3},{7,5},{... | collective-permute-start | bytes 589832 | tf_op jit(solution)/shard_map/ppermute | solution.py:15
  74.3 3.1 collective-permute-start.5
  81.7 5.9 %collective-permute-start.7 = (f32[1,3,2,1,32,256]{5,4,3,2,1,0:T(8,128)S(1)}, f32[1,3,2,1,32,256]{5,4,3,2,1,0:T(8,128)S(1)}, u32[]{:S(2)}, u32[]{:S(2)}) collective-permute-start(f32[1,3,2,1,32,256]{5,4,3,2,1,0:T(8,128)S(1)} %pad_maximum_fusion.31), channel_id=1, source_target_pairs={{0,2},{2,4},{4,6},{6,8},{8,10},{10,12},{12,14},{1,3},{3,5},{5,7},{... | collective-permute-start | bytes 589832 | tf_op jit(solution)/shard_map/ppermute | solution.py:15
  83.2 4.4 collective-permute-start.6
  163.9 8.6 %collective-permute-start.8 = (f32[1,3,2,1,32,256]{5,4,3,2,1,0:T(8,128)S(1)}, f32[1,3,2,1,32,256]{5,4,3,2,1,0:T(8,128)S(1)}, u32[]{:S(2)}, u32[]{:S(2)}) collective-permute-start(f32[1,3,2,1,32,256]{5,4,3,2,1,0:T(8,128)S(1)} %slice.2170), channel_id=1, source_target_pairs={{2,0},{4,2},{6,4},{8,6},{10,8},{12,10},{14,12},{3,1},{5,3},{7,5},{... | collective-permute-start | bytes 589832 | tf_op jit(solution)/shard_map/ppermute | solution.py:15
  165.2 3.1 collective-permute-start.9
  173.6 4.9 %collective-permute-start.11 = (f32[1,3,2,1,32,256]{5,4,3,2,1,0:T(8,128)S(1)}, f32[1,3,2,1,32,256]{5,4,3,2,1,0:T(8,128)S(1)}, u32[]{:S(2)}, u32[]{:S(2)}) collective-permute-start(f32[1,3,2,1,32,256]{5,4,3,2,1,0:T(8,128)S(1)} %pad_maximum_fusion.29), channel_id=1, source_target_pairs={{0,2},{2,4},{4,6},{6,8},{8,10},{10,12},{12,14},{1,3},{3,5},{5,7},{... | collective-permute-start | bytes 589832 | tf_op jit(solution)/shard_map/ppermute | solution.py:15
  175.1 2.1 collective-permute-start.10
  225.6 7.8 %collective-permute-start.12 = (f32[1,3,2,1,32,256]{5,4,3,2,1,0:T(8,128)S(1)}, f32[1,3,2,1,32,256]{5,4,3,2,1,0:T(8,128)S(1)}, u32[]{:S(2)}, u32[]{:S(2)}) collective-permute-start(f32[1,3,2,1,32,256]{5,4,3,2,1,0:T(8,128)S(1)} %slice.2211), channel_id=1, source_target_pairs={{2,0},{4,2},{6,4},{8,6},{10,8},{12,10},{14,12},{3,1},{5,3},{7,5},{... | collective-permute-start | bytes 589832 | tf_op jit(solution)/shard_map/ppermute | solution.py:15
  226.9 3.1 collective-permute-start.13
  235.0 5.6 %collective-permute-start.15 = (f32[1,3,2,1,32,256]{5,4,3,2,1,0:T(8,128)S(1)}, f32[1,3,2,1,32,256]{5,4,3,2,1,0:T(8,128)S(1)}, u32[]{:S(2)}, u32[]{:S(2)}) collective-permute-start(f32[1,3,2,1,32,256]{5,4,3,2,1,0:T(8,128)S(1)} %pad_maximum_fusion.27), channel_id=1, source_target_pairs={{0,2},{2,4},{4,6},{6,8},{8,10},{10,12},{12,14},{1,3},{3,5},{5,7},{... | collective-permute-start | bytes 589832 | tf_op jit(solution)/shard_map/ppermute | solution.py:15
  236.5 4.0 collective-permute-start.14
  323.3 8.1 %collective-permute-start.16 = (f32[1,3,2,1,32,256]{5,4,3,2,1,0:T(8,128)S(1)}, f32[1,3,2,1,32,256]{5,4,3,2,1,0:T(8,128)S(1)}, u32[]{:S(2)}, u32[]{:S(2)}) collective-permute-start(f32[1,3,2,1,32,256]{5,4,3,2,1,0:T(8,128)S(1)} %slice.2254), channel_id=1, source_target_pairs={{2,0},{4,2},{6,4},{8,6},{10,8},{12,10},{14,12},{3,1},{5,3},{7,5},{... | collective-permute-start | bytes 589832 | tf_op jit(solution)/shard_map/ppermute | solution.py:15
  324.6 3.1 collective-permute-start.17
  333.0 5.3 %collective-permute-start.19 = (f32[1,3,2,1,32,256]{5,4,3,2,1,0:T(8,128)S(1)}, f32[1,3,2,1,32,256]{5,4,3,2,1,0:T(8,128)S(1)}, u32[]{:S(2)}, u32[]{:S(2)}) collective-permute-start(f32[1,3,2,1,32,256]{5,4,3,2,1,0:T(8,128)S(1)} %pad_maximum_fusion.25), channel_id=1, source_target_pairs={{0,2},{2,4},{4,6},{6,8},{8,10},{10,12},{12,14},{1,3},{3,5},{5,7},{... | collective-permute-start | bytes 589832 | tf_op jit(solution)/shard_map/ppermute | solution.py:15
  334.6 2.1 collective-permute-start.18
  393.0 5.0 %collective-permute-start.21 = (f32[1,3,2,4,1,256]{5,4,3,2,1,0:T(1,128)S(1)}, f32[1,3,2,4,1,256]{5,4,3,2,1,0:T(1,128)S(1)}, u32[]{:S(2)}, u32[]{:S(2)}) collective-permute-start(f32[1,3,2,4,1,256]{5,4,3,2,1,0:T(1,128)S(1)} %slice.2299), channel_id=1, source_target_pairs={{1,0},{3,2},{5,4},{7,6},{9,8},{11,10},{13,12},{15,14},{17,16},{19,... | collective-permute-start | bytes 73736 | tf_op jit(solution)/shard_map/ppermute | solution.py:15
  394.3 9.5 %collective-permute-start.20 = (f32[1,3,2,1,32,256]{5,4,3,2,1,0:T(8,128)S(1)}, f32[1,3,2,1,32,256]{5,4,3,2,1,0:T(8,128)S(1)}, u32[]{:S(2)}, u32[]{:S(2)}) collective-permute-start(f32[1,3,2,1,32,256]{5,4,3,2,1,0:T(8,128)S(1)} %slice.2295), channel_id=1, source_target_pairs={{2,0},{4,2},{6,4},{8,6},{10,8},{12,10},{14,12},{3,1},{5,3},{7,5},{... | collective-permute-start | bytes 589832 | tf_op jit(solution)/shard_map/ppermute | solution.py:15
  405.4 6.1 %collective-permute-start.22 = (f32[1,3,2,4,1,256]{5,4,3,2,1,0:T(1,128)S(1)}, f32[1,3,2,4,1,256]{5,4,3,2,1,0:T(1,128)S(1)}, u32[]{:S(2)}, u32[]{:S(2)}) collective-permute-start(f32[1,3,2,4,1,256]{5,4,3,2,1,0:T(1,128)S(1)} %pad_maximum_fusion.35), channel_id=1, source_target_pairs={{0,1},{2,3},{4,5},{6,7},{8,9},{10,11},{12,13},{14,15},{16,17},{18,... | collective-permute-start | bytes 73736 | tf_op jit(solution)/shard_map/ppermute | solution.py:15
  407.5 5.3 %collective-permute-start.23 = (f32[1,3,2,1,32,256]{5,4,3,2,1,0:T(8,128)S(1)}, f32[1,3,2,1,32,256]{5,4,3,2,1,0:T(8,128)S(1)}, u32[]{:S(2)}, u32[]{:S(2)}) collective-permute-start(f32[1,3,2,1,32,256]{5,4,3,2,1,0:T(8,128)S(1)} %pad_maximum_fusion.23), channel_id=1, source_target_pairs={{0,2},{2,4},{4,6},{6,8},{8,10},{10,12},{12,14},{1,3},{3,5},{5,7},{... | collective-permute-start | bytes 589832 | tf_op jit(solution)/shard_map/ppermute | solution.py:15
  (78 other events, 651.4 us)
where the time goes:
time: 472 us; the launch traced here: 469 us
  blocking collectives  181 us (38%)
  between operations  99.9 us (21%)
  other arithmetic  74.5 us (16%)
  waiting for transfers between devices  43.6 us (9%)
  starting transfers between devices  38.4 us (8%)
  local copies, waits for them, and re-layouts  31.8 us (7%)
    psum x3, blocking collectives, body(): lax.psum((product(second, middle), product(second, second), product(sourc...  89.6 us
    psum x2, blocking collectives, body(): lax.psum(product(source, applied), ('gx', 'gy'))  60.3 us
    ppermute x24, waiting for transfers between devices, shifted(): return lax.ppermute(array, axis, pairs)  43.6 us
    ppermute x24, starting transfers between devices, shifted(): return lax.ppermute(array, axis, pairs)  38.4 us
    psum x1, blocking collectives, body(): shadow_dot = lax.psum(product(source, residual), ('gx', 'gy'))  31.3 us
    sub x15, other arithmetic, scaled(): real_part = values[:, :, 0] * real_scale - values[:, :, 1] * imag_scale  27.3 us
    another operation x12, other arithmetic, product(): return jnp.stack([real_part, imag_part])  17.5 us
    unnamed x173, local copies, waits for them, and re-layouts  12.9 us
  transfers between devices with their start and end apart: 24, of which 17 were waited for; matrix products, arithmetic and copies ran while one was open for 2% of the time, Pallas kernels for 0%

commit v1 on v0

--- a/solution.py
+++ b/solution.py
@@ -151,7 +151,8 @@
     solution = jnp.zeros_like(source)
     residual = source
     direction = source
-    shadow_dot = lax.psum(product(source, residual), ("gx", "gy"))
+    u_in = product(source, residual)
+    shadow_dot = lax.psum(lax.psum(u_in, "gy"), "gx")
     for iteration in range(ITERS):
         applied = operate(direction)
         step_size = complex_ratio(shadow_dot, lax.psum(product(source, applied), ("gx", "gy")))

time: 472 us -> 493 us (1.044)
  blocking collectives: 181 us -> 201 us
    psum x2 -> x3, blocking collectives: 60.3 us -> 91.6 us  [body(): lax.psum(product(source, applied), ('gx', 'gy'))]
    psum x1 -> x2, blocking collectives: 31.3 us -> 19.6 us  [body(): shadow_dot = lax.psum(lax.psum(u_in, 'gy'), 'gx')]
  transfers between devices with their start and end apart: 24 -> 24, of which waited for: 17 -> 17; matrix products, arithmetic and copies ran while one was open for 2% -> 1% of each run, Pallas kernels for 0% -> 0%
where the time goes in v1:
time: 493 us; the launch traced here: 490 us
  blocking collectives  201 us (41%)
  between operations  98 us (20%)
  other arithmetic  74.2 us (15%)
  waiting for transfers between devices  43.7 us (9%)
  starting transfers between devices  41.3 us (8%)
  local copies, waits for them, and re-layouts  31.6 us (6%)
    psum x3, blocking collectives, body(): lax.psum(product(source, applied), ('gx', 'gy'))  91.6 us
    psum x3, blocking collectives, body(): lax.psum((product(second, middle), product(second, second), product(sourc...  89.6 us
    ppermute x24, waiting for transfers between devices, shifted(): return lax.ppermute(array, axis, pairs)  43.7 us
    ppermute x24, starting transfers between devices, shifted(): return lax.ppermute(array, axis, pairs)  41.3 us
    sub x15, other arithmetic, scaled(): real_part = values[:, :, 0] * real_scale - values[:, :, 1] * imag_scale  27 us
    psum x2, blocking collectives, body(): shadow_dot = lax.psum(lax.psum(u_in, 'gy'), 'gx')  19.6 us
    another operation x12, other arithmetic, product(): return jnp.stack([real_part, imag_part])  17.5 us
    unnamed x173, local copies, waits for them, and re-layouts  13 us
  transfers between devices with their start and end apart: 24, of which 17 were waited for; matrix products, arithmetic and copies ran while one was open for 1% of the time, Pallas kernels for 0%

profile of v1, /device:TPU:0, one launch (start us, length us, event | category | flops | bytes accessed | tf_op | source)
XLA Modules:
  0.0 489.5 jit_solution(8392014566516099603)
XLA Ops:
  7.5 6.7 %collective-permute-done = f32[1,3,2,1,32,256]{5,4,3,2,1,0:T(8,128)S(1)} collective-permute-done((f32[1,3,2,1,32,256]{5,4,3,2,1,0:T(8,128)S(1)}, f32[1,3,2,1,32,256]{5,4,3,2,1,0:T(8,128)S(1)}, u32[]{:S(2)}, u32[]{:S(2)}) %collective-permute-start) | collective-permute-done | bytes 196640 | tf_op jit(solution)/shard_map/ppermute | solution.py:15
  15.4 2.2 collective-permute-start.2
  17.5 5.0 %collective-permute-start.3 = (f32[1,3,2,1,32,256]{5,4,3,2,1,0:T(8,128)S(1)}, f32[1,3,2,1,32,256]{5,4,3,2,1,0:T(8,128)S(1)}, u32[]{:S(2)}, u32[]{:S(2)}) collective-permute-start(f32[1,3,2,1,32,256]{5,4,3,2,1,0:T(8,128)S(1)} %pad_maximum_fusion.33), channel_id=1, source_target_pairs={{0,2},{2,4},{4,6},{6,8},{8,10},{10,12},{12,14},{1,3},{3,5},{5,7},{... | collective-permute-start | bytes 589832 | tf_op jit(solution)/shard_map/ppermute | solution.py:15
  22.5 3.6 collective-permute-done.3
  29.8 31.3 %psum.93 = f32[2,1]{1,0:T(2,128)S(1)} all-reduce(f32[2,1]{1,0:T(2,128)S(1)} %pad_maximum_fusion.42), channel_id=1, replica_groups=mesh['groups'=2,'gx'=8,'gy'=2] {'gx','gy'}, use_global_device_ids=true, to_apply=%region_6.0 | all-reduce | flops 2 | bytes 16 | tf_op jit(solution)/shard_map/psum | solution.py:158
  64.1 2.5 psum.91
  67.9 17.1 %psum.92 = f32[2,1]{1,0:T(2,128)S(1)} all-reduce(f32[2,1]{1,0:T(2,128)S(1)} %psum.91), channel_id=1, replica_groups=mesh['groups'=2,'gx'=8,'gy'=2] {'gx'}, use_global_device_ids=true, to_apply=%region_3.0 | all-reduce | flops 2 | bytes 16 | tf_op jit(solution)/shard_map/psum | solution.py:155
  97.3 3.2 collective-permute-done.4
  101.6 4.8 collective-permute-start.7
  117.6 29.5 %all-reduce.38 = (f32[2,1]{1,0:T(2,128)S(1)}, f32[2,1]{1,0:T(2,128)S(1)}, f32[2,1]{1,0:T(2,128)S(1)}) all-reduce(f32[2,1]{1,0:T(2,128)S(1)} %pad_maximum_fusion.43, f32[2,1]{1,0:T(2,128)S(1)} %pad_maximum_fusion.44, f32[2,1]{1,0:T(2,128)S(1)} %pad_maximum_fusion.45), channel_id=1, replica_groups=mesh['groups'=2,'gx'=8,'gy'=2] {'gx','gy'}, use_global_device_ids=true, to_apply=%region_9.0 | all-reduce | flops 6 | bytes 48 | tf_op jit(solution)/shard_map/psum | solution.py:161
  163.1 2.4 multiply_subtract_fusion.11
  189.0 4.2 collective-permute-done.8
  204.0 30.3 %psum.97 = f32[2,1]{1,0:T(2,128)S(1)} all-reduce(f32[2,1]{1,0:T(2,128)S(1)} %pad_maximum_fusion.46), channel_id=1, replica_groups=mesh['groups'=2,'gx'=8,'gy'=2] {'gx','gy'}, use_global_device_ids=true, to_apply=%region_18.0 | all-reduce | flops 2 | bytes 16 | tf_op jit(solution)/shard_map/psum | solution.py:158
  242.9 2.5 multiply_subtract_fusion.8
  250.2 3.4 collective-permute-done.12
  267.7 1.9 pad_maximum_fusion.48
  269.6 2.0 pad_maximum_fusion.47
  271.6 30.6 %all-reduce.37 = (f32[2,1]{1,0:T(2,128)}, f32[2,1]{1,0:T(2,128)}, f32[2,1]{1,0:T(2,128)}) all-reduce(f32[2,1]{1,0:T(2,128)} %pad_maximum_fusion.47, f32[2,1]{1,0:T(2,128)} %pad_maximum_fusion.48, f32[2,1]{1,0:T(2,128)} %pad_maximum_fusion.49), channel_id=1, replica_groups=mesh['groups'=2,'gx'=8,'gy'=2] {'gx','gy'}, use_global_device_ids=true, to_apply=%region_21.0 | all-reduce | flops 6 | bytes 48 | tf_op jit(solution)/shard_map/psum | solution.py:161
  320.6 2.5 multiply_subtract_fusion.5
  348.1 3.7 collective-permute-done.16
  362.8 3.0 add_reduce_fusion.2
  367.5 2.2 multiply_subtract_fusion.13
  369.7 30.0 %psum.101 = f32[2,1]{1,0:T(2,128)S(1)} all-reduce(f32[2,1]{1,0:T(2,128)} %pad_maximum_fusion.50), channel_id=1, replica_groups=mesh['groups'=2,'gx'=8,'gy'=2] {'gx','gy'}, use_global_device_ids=true, to_apply=%region_30.0 | all-reduce | flops 2 | bytes 16 | tf_op jit(solution)/shard_map/psum | solution.py:158
  408.2 2.5 multiply_subtract_fusion.2
  410.8 2.3 maximum_subtract_fusion.11
  415.7 2.3 multiply_subtract_fusion.9
  418.0 5.9 %collective-permute-done.20 = f32[1,3,2,1,32,256]{5,4,3,2,1,0:T(8,128)S(1)} collective-permute-done((f32[1,3,2,1,32,256]{5,4,3,2,1,0:T(8,128)S(1)}, f32[1,3,2,1,32,256]{5,4,3,2,1,0:T(8,128)S(1)}, u32[]{:S(2)}, u32[]{:S(2)}) %collective-permute-start.20) | collective-permute-done | bytes 196640 | tf_op jit(solution)/shard_map/ppermute | solution.py:15
  425.6 2.0 collective-permute-start.22
  429.5 2.2 multiply_subtract_fusion.7
  441.1 2.3 multiply_subtract_fusion.3
  443.4 29.5 %all-reduce.36 = (f32[2,1]{1,0:T(2,128)S(1)}, f32[2,1]{1,0:T(2,128)S(1)}) all-reduce(f32[2,1]{1,0:T(2,128)S(1)} %pad_maximum_fusion.51, f32[2,1]{1,0:T(2,128)S(1)} %pad_maximum_fusion.52), channel_id=1, replica_groups=mesh['groups'=2,'gx'=8,'gy'=2] {'gx','gy'}, use_global_device_ids=true, to_apply=%region_33.0 | all-reduce | flops 4 | bytes 32 | tf_op jit(solution)/shard_map/psum | solution.py:161
  481.8 2.6 multiply_subtract_fusion
  (457 shorter events, 115.5 us)
Async XLA Ops:
  1.6 12.5 %collective-permute-start.1 = (f32[1,3,2,4,1,256]{5,4,3,2,1,0:T(1,128)S(1)}, f32[1,3,2,4,1,256]{5,4,3,2,1,0:T(1,128)S(1)}, u32[]{:S(2)}, u32[]{:S(2)}) collective-permute-start(f32[1,3,2,4,1,256]{5,4,3,2,1,0:T(1,128)S(1)} %slice.702), channel_id=1, source_target_pairs={{1,0},{3,2},{5,4},{7,6},{9,8},{11,10},{13,12},{15,14},{17,16},{19,... | collective-permute-start | bytes 73736 | tf_op jit(solution)/shard_map/ppermute | solution.py:15
  3.9 10.2 %collective-permute-start = (f32[1,3,2,1,32,256]{5,4,3,2,1,0:T(8,128)S(1)}, f32[1,3,2,1,32,256]{5,4,3,2,1,0:T(8,128)S(1)}, u32[]{:S(2)}, u32[]{:S(2)}) collective-permute-start(f32[1,3,2,1,32,256]{5,4,3,2,1,0:T(8,128)S(1)} %slice.695), channel_id=1, source_target_pairs={{2,0},{4,2},{6,4},{8,6},{10,8},{12,10},{14,12},{3,1},{5,3},{7,5},{... | collective-permute-start | bytes 589832 | tf_op jit(solution)/shard_map/ppermute | solution.py:15
  7.1 192.8 %copy-start.53 = (f32[4]{0:T(128)}, f32[4]{0:T(128)S(1)}, u32[]{:S(2)}) copy-start(f32[4]{0:T(128)S(1)} %get-tuple-element.422) | copy-start | bytes 52
  7.1 192.8 %copy-start.57 = (f32[4]{0:T(128)}, f32[4]{0:T(128)S(1)}, u32[]{:S(2)}) copy-start(f32[4]{0:T(128)S(1)} %get-tuple-element.423) | copy-start | bytes 52
  7.2 186.9 %copy-start.61 = (f32[4]{0:T(128)}, f32[4]{0:T(128)S(1)}, u32[]{:S(2)}) copy-start(f32[4]{0:T(128)S(1)} %get-tuple-element.430) | copy-start | bytes 52
  7.2 186.9 %copy-start.65 = (f32[4]{0:T(128)}, f32[4]{0:T(128)S(1)}, u32[]{:S(2)}) copy-start(f32[4]{0:T(128)S(1)} %get-tuple-element.431) | copy-start | bytes 52
  7.4 193.0 %copy-start.16 = (f32[3,4,32,256]{3,2,1,0:T(8,128)}, f32[3,4,32,256]{3,2,1,0:T(8,128)S(1)}, u32[]{:S(2)}) copy-start(f32[3,4,32,256]{3,2,1,0:T(8,128)S(1)} %broadcast_multiply_fusion) | copy-start | bytes 1179652
  7.4 186.4 %copy-start.77 = (f32[32]{0:T(128)}, f32[32]{0:T(128)S(1)}, u32[]{:S(2)}) copy-start(f32[32]{0:T(128)S(1)} %get-tuple-element.428) | copy-start | bytes 388
  7.4 186.4 %copy-start.81 = (f32[32]{0:T(128)}, f32[32]{0:T(128)S(1)}, u32[]{:S(2)}) copy-start(f32[32]{0:T(128)S(1)} %get-tuple-element.429) | copy-start | bytes 388
  15.4 7.2 %collective-permute-start.2 = (f32[1,3,2,4,1,256]{5,4,3,2,1,0:T(1,128)S(1)}, f32[1,3,2,4,1,256]{5,4,3,2,1,0:T(1,128)S(1)}, u32[]{:S(2)}, u32[]{:S(2)}) collective-permute-start(f32[1,3,2,4,1,256]{5,4,3,2,1,0:T(1,128)S(1)} %pad_maximum_fusion.40), channel_id=1, source_target_pairs={{0,1},{2,3},{4,5},{6,7},{8,9},{10,11},{12,13},{14,15},{16,17},{18,... | collective-permute-start | bytes 73736 | tf_op jit(solution)/shard_map/ppermute | solution.py:15
  17.5 8.7 %collective-permute-start.3 = (f32[1,3,2,1,32,256]{5,4,3,2,1,0:T(8,128)S(1)}, f32[1,3,2,1,32,256]{5,4,3,2,1,0:T(8,128)S(1)}, u32[]{:S(2)}, u32[]{:S(2)}) collective-permute-start(f32[1,3,2,1,32,256]{5,4,3,2,1,0:T(8,128)S(1)} %pad_maximum_fusion.33), channel_id=1, source_target_pairs={{0,2},{2,4},{4,6},{6,8},{8,10},{10,12},{12,14},{1,3},{3,5},{5,7},{... | collective-permute-start | bytes 589832 | tf_op jit(solution)/shard_map/ppermute | solution.py:15
  22.5 177.5 %copy-start.69 = (f32[32]{0:T(128)}, f32[32]{0:T(128)S(1)}, u32[]{:S(2)}) copy-start(f32[32]{0:T(128)S(1)} %get-tuple-element.420) | copy-start | bytes 388
  92.9 7.6 %collective-permute-start.4 = (f32[1,3,2,1,32,256]{5,4,3,2,1,0:T(8,128)S(1)}, f32[1,3,2,1,32,256]{5,4,3,2,1,0:T(8,128)S(1)}, u32[]{:S(2)}, u32[]{:S(2)}) collective-permute-start(f32[1,3,2,1,32,256]{5,4,3,2,1,0:T(8,128)S(1)} %slice.2127), channel_id=1, source_target_pairs={{2,0},{4,2},{6,4},{8,6},{10,8},{12,10},{14,12},{3,1},{5,3},{7,5},{... | collective-permute-start | bytes 589832 | tf_op jit(solution)/shard_map/ppermute | solution.py:15
  94.2 3.1 collective-permute-start.5
  101.6 8.7 %collective-permute-start.7 = (f32[1,3,2,1,32,256]{5,4,3,2,1,0:T(8,128)S(1)}, f32[1,3,2,1,32,256]{5,4,3,2,1,0:T(8,128)S(1)}, u32[]{:S(2)}, u32[]{:S(2)}) collective-permute-start(f32[1,3,2,1,32,256]{5,4,3,2,1,0:T(8,128)S(1)} %pad_maximum_fusion.31), channel_id=1, source_target_pairs={{0,2},{2,4},{4,6},{6,8},{8,10},{10,12},{12,14},{1,3},{3,5},{5,7},{... | collective-permute-start | bytes 589832 | tf_op jit(solution)/shard_map/ppermute | solution.py:15
  106.4 3.8 collective-permute-start.6
  184.6 8.6 %collective-permute-start.8 = (f32[1,3,2,1,32,256]{5,4,3,2,1,0:T(8,128)S(1)}, f32[1,3,2,1,32,256]{5,4,3,2,1,0:T(8,128)S(1)}, u32[]{:S(2)}, u32[]{:S(2)}) collective-permute-start(f32[1,3,2,1,32,256]{5,4,3,2,1,0:T(8,128)S(1)} %slice.2170), channel_id=1, source_target_pairs={{2,0},{4,2},{6,4},{8,6},{10,8},{12,10},{14,12},{3,1},{5,3},{7,5},{... | collective-permute-start | bytes 589832 | tf_op jit(solution)/shard_map/ppermute | solution.py:15
  185.9 3.1 collective-permute-start.9
  194.3 4.9 collective-permute-start.11
  195.8 2.1 collective-permute-start.10
  245.8 7.8 %collective-permute-start.12 = (f32[1,3,2,1,32,256]{5,4,3,2,1,0:T(8,128)S(1)}, f32[1,3,2,1,32,256]{5,4,3,2,1,0:T(8,128)S(1)}, u32[]{:S(2)}, u32[]{:S(2)}) collective-permute-start(f32[1,3,2,1,32,256]{5,4,3,2,1,0:T(8,128)S(1)} %slice.2211), channel_id=1, source_target_pairs={{2,0},{4,2},{6,4},{8,6},{10,8},{12,10},{14,12},{3,1},{5,3},{7,5},{... | collective-permute-start | bytes 589832 | tf_op jit(solution)/shard_map/ppermute | solution.py:15
  247.1 3.1 collective-permute-start.13
  255.2 5.6 %collective-permute-start.15 = (f32[1,3,2,1,32,256]{5,4,3,2,1,0:T(8,128)S(1)}, f32[1,3,2,1,32,256]{5,4,3,2,1,0:T(8,128)S(1)}, u32[]{:S(2)}, u32[]{:S(2)}) collective-permute-start(f32[1,3,2,1,32,256]{5,4,3,2,1,0:T(8,128)S(1)} %pad_maximum_fusion.27), channel_id=1, source_target_pairs={{0,2},{2,4},{4,6},{6,8},{8,10},{10,12},{12,14},{1,3},{3,5},{5,7},{... | collective-permute-start | bytes 589832 | tf_op jit(solution)/shard_map/ppermute | solution.py:15
  256.7 3.9 collective-permute-start.14
  343.7 8.1 %collective-permute-start.16 = (f32[1,3,2,1,32,256]{5,4,3,2,1,0:T(8,128)S(1)}, f32[1,3,2,1,32,256]{5,4,3,2,1,0:T(8,128)S(1)}, u32[]{:S(2)}, u32[]{:S(2)}) collective-permute-start(f32[1,3,2,1,32,256]{5,4,3,2,1,0:T(8,128)S(1)} %slice.2254), channel_id=1, source_target_pairs={{2,0},{4,2},{6,4},{8,6},{10,8},{12,10},{14,12},{3,1},{5,3},{7,5},{... | collective-permute-start | bytes 589832 | tf_op jit(solution)/shard_map/ppermute | solution.py:15
  345.1 3.1 collective-permute-start.17
  353.5 5.3 %collective-permute-start.19 = (f32[1,3,2,1,32,256]{5,4,3,2,1,0:T(8,128)S(1)}, f32[1,3,2,1,32,256]{5,4,3,2,1,0:T(8,128)S(1)}, u32[]{:S(2)}, u32[]{:S(2)}) collective-permute-start(f32[1,3,2,1,32,256]{5,4,3,2,1,0:T(8,128)S(1)} %pad_maximum_fusion.25), channel_id=1, source_target_pairs={{0,2},{2,4},{4,6},{6,8},{8,10},{10,12},{12,14},{1,3},{3,5},{5,7},{... | collective-permute-start | bytes 589832 | tf_op jit(solution)/shard_map/ppermute | solution.py:15
  355.0 2.1 collective-permute-start.18
  413.1 4.9 %collective-permute-start.21 = (f32[1,3,2,4,1,256]{5,4,3,2,1,0:T(1,128)S(1)}, f32[1,3,2,4,1,256]{5,4,3,2,1,0:T(1,128)S(1)}, u32[]{:S(2)}, u32[]{:S(2)}) collective-permute-start(f32[1,3,2,4,1,256]{5,4,3,2,1,0:T(1,128)S(1)} %slice.2299), channel_id=1, source_target_pairs={{1,0},{3,2},{5,4},{7,6},{9,8},{11,10},{13,12},{15,14},{17,16},{19,... | collective-permute-start | bytes 73736 | tf_op jit(solution)/shard_map/ppermute | solution.py:15
  414.4 9.5 %collective-permute-start.20 = (f32[1,3,2,1,32,256]{5,4,3,2,1,0:T(8,128)S(1)}, f32[1,3,2,1,32,256]{5,4,3,2,1,0:T(8,128)S(1)}, u32[]{:S(2)}, u32[]{:S(2)}) collective-permute-start(f32[1,3,2,1,32,256]{5,4,3,2,1,0:T(8,128)S(1)} %slice.2295), channel_id=1, source_target_pairs={{2,0},{4,2},{6,4},{8,6},{10,8},{12,10},{14,12},{3,1},{5,3},{7,5},{... | collective-permute-start | bytes 589832 | tf_op jit(solution)/shard_map/ppermute | solution.py:15
  425.6 6.1 %collective-permute-start.22 = (f32[1,3,2,4,1,256]{5,4,3,2,1,0:T(1,128)S(1)}, f32[1,3,2,4,1,256]{5,4,3,2,1,0:T(1,128)S(1)}, u32[]{:S(2)}, u32[]{:S(2)}) collective-permute-start(f32[1,3,2,4,1,256]{5,4,3,2,1,0:T(1,128)S(1)} %pad_maximum_fusion.35), channel_id=1, source_target_pairs={{0,1},{2,3},{4,5},{6,7},{8,9},{10,11},{12,13},{14,15},{16,17},{18,... | collective-permute-start | bytes 73736 | tf_op jit(solution)/shard_map/ppermute | solution.py:15
  427.6 5.3 %collective-permute-start.23 = (f32[1,3,2,1,32,256]{5,4,3,2,1,0:T(8,128)S(1)}, f32[1,3,2,1,32,256]{5,4,3,2,1,0:T(8,128)S(1)}, u32[]{:S(2)}, u32[]{:S(2)}) collective-permute-start(f32[1,3,2,1,32,256]{5,4,3,2,1,0:T(8,128)S(1)} %pad_maximum_fusion.23), channel_id=1, source_target_pairs={{0,2},{2,4},{4,6},{6,8},{8,10},{10,12},{12,14},{1,3},{3,5},{5,7},{... | collective-permute-start | bytes 589832 | tf_op jit(solution)/shard_map/ppermute | solution.py:15
  (78 other events, 690.1 us)
